TPU v7x, 32 devices: a whole 2x2x4 slice. The times are simulated.
32 devices in a mesh: grp: 4 (over z), gx: 8 (over y, x, core).
Axes of the slice: x: 2, y: 2, z: 4, core: 2. Of those that a mesh axis runs over, the one named last changes fastest.
Arguments:
- component_density: float32 [53, 256, 1024], P(None, 'gx', 'grp'), may hold values from 0.05 to 2
- scaled_thermal_state: float32 [256, 1024], P('gx', 'grp'), may hold values from 0.5 to 1.5
- leading_direction_flow: float32 [256, 1024], P('gx', 'grp'), may hold values from -1 to 1
- trailing_direction_flow: float32 [256, 1024], P('gx', 'grp'), may hold values from -1 to 1
- spreading_coefficient: float32 [54], replicated, may hold values from 0.02 to 0.2
- colliding_pair: int32 [325, 2], replicated, may hold values from 0 to 52
- natural_exponent_scaler: float32 [325], replicated, may hold values from -3 to -1
- arrhenius_energy: float32 [325], replicated, may hold values from 0 to 2
- stoichiometric_output: float32 [325, 53], replicated, may hold values from 0.004 to 0.075
- formation_warming: float32 [53], replicated, may hold values from -1.8 to 1.8
- explicit_increments: int32 [2048], P(('grp', 'gx')), may hold values from 1 to 4
Outputs:
- species_out: float32 [53, 256, 1024], P(None, 'gx', 'grp')
- temperature_out: float32 [256, 1024], P('gx', 'grp')
All inputs are finite; a program needn't handle non-finite values.
Results may differ from a plain program's by a relative error of at most 0.0003.
Values sent between devices are 32-bit elements; how exact they have to be, the bound alone decides.
A program may use at most 64 MiB of HBM per device.

v0:
```python
import functools
import math

import jax
import jax.numpy as jnp
import numpy as np
from jax import lax
from jax.experimental import pallas as pl
from jax.experimental.pallas import tpu as pltpu
from jax.sharding import PartitionSpec as P

TILE = 128
HALO = 9
FIRST_SCALE = 60.0
SECOND_SCALE = 180.0
transport_step = 0.4
chemistry_span = 0.5
sixth_first = (0.75, -0.15, 1.0 / 60.0)
sixth_second = (1.5, -0.15, 1.0 / 90.0)
sixth_center = -49.0 / 18.0


def up8(n):
    return -(-n // 8) * 8


def halo_kernel(sizes, main, first_cols, last_cols, top, bottom, left, right, send, recv):
    n_grp, n_gx = sizes
    g, x = lax.axis_index("grp"), lax.axis_index("gx")
    rows = main.shape[0]
    place = lambda dg, dx: (lax.rem(g + dg + n_grp, n_grp), lax.rem(x + dx + n_gx, n_gx))
    barrier = pltpu.get_barrier_semaphore()
    around = [(dg, dx) for dg in (-1, 0, 1) for dx in (-1, 0, 1) if (dg, dx) != (0, 0)]
    for dg, dx in around:
        pl.semaphore_signal(barrier, inc=1, device_id=place(dg, dx),
                            device_id_type=pl.DeviceIdType.MESH)
    pl.semaphore_wait(barrier, len(around))
    early, late = pl.ds(0, HALO), pl.ds(rows - HALO, HALO)
    above, beside, below = pl.ds(0, HALO), pl.ds(HALO, rows), pl.ds(HALO + rows, HALO)
    plan = [
        (main.at[late], top, 0, 1),
        (main.at[early], bottom, 0, -1),
        (last_cols, left.at[beside], 1, 0),
        (first_cols, right.at[beside], -1, 0),
        (last_cols.at[late], left.at[above], 1, 1),
        (last_cols.at[early], left.at[below], 1, -1),
        (first_cols.at[late], right.at[above], -1, 1),
        (first_cols.at[early], right.at[below], -1, -1),
    ]
    copies = []
    for n, (src, dst, dg, dx) in enumerate(plan):
        copy = pltpu.make_async_remote_copy(
            src_ref=src, dst_ref=dst, send_sem=send.at[n], recv_sem=recv.at[n],
            device_id=place(dg, dx), device_id_type=pl.DeviceIdType.MESH)
        copy.start()
        copies.append(copy)
    for copy in copies:
        copy.wait()


def exchange(main, first_cols, last_cols):
    rows, layers, cols = main.shape
    sizes = (lax.axis_size("grp"), lax.axis_size("gx"))
    anywhere = pl.BlockSpec(memory_space=pltpu.VMEM)
    strip = jax.ShapeDtypeStruct((HALO, layers, cols), jnp.float32)
    edge = jax.ShapeDtypeStruct((rows + 2 * HALO,) + first_cols.shape[1:], jnp.float32)
    return pl.pallas_call(
        functools.partial(halo_kernel, sizes),
        in_specs=[anywhere] * 3,
        out_specs=[anywhere] * 4,
        out_shape=[strip, strip, edge, edge],
        scratch_shapes=[pltpu.SemaphoreType.DMA((8,)), pltpu.SemaphoreType.DMA((8,))],
        compiler_params=pltpu.CompilerParams(collective_id=0, has_side_effects=True),
        name="halo",
    )(main, first_cols, last_cols)


def halves(value):
    high = value.astype(jnp.bfloat16)
    return high, (value - high.astype(jnp.float32)).astype(jnp.bfloat16)


def transport_kernel(fields, main, top, bottom, side, diff, band, uv_main, uv_top, uv_bottom, uv_side,
                     out, start, one, two, east, north, pieces, across):
    rows, _, cols = main.shape
    wide = rows + 2 * HALO
    gap = side.shape[2]
    width = cols + gap
    tile = pl.program_id(0)
    u_at, v_at = fields % 8, (fields + 1) % 8

    def fill(dst, m, t, b, s, sub):
        def put(r, ref, at):
            if sub is None:
                dst[r, :, :cols] = ref[at]
            else:
                dst[r, :, :cols] = jnp.broadcast_to(ref[at, sub:sub + 1, :], (8, cols))

        def mid(r, c):
            put(HALO + r, m, r)
            return c

        lax.fori_loop(0, rows, mid, 0, unroll=4)
        for r in range(HALO):
            put(r, t, r)
            put(HALO + rows + r, b, r)

        def edge(r, c):
            if sub is None:
                dst[r, :, cols:] = s[r]
            else:
                dst[r, :, cols:] = jnp.broadcast_to(s[r, sub:sub + 1, :], (8, gap))
            return c

        lax.fori_loop(0, wide, edge, 0, unroll=5)

    @pl.when(tile == 0)
    def _():
        fill(east, uv_main, uv_top, uv_bottom, uv_side, u_at)
        fill(north, uv_main, uv_top, uv_bottom, uv_side, v_at)

    fill(start, main, top, bottom, side, None)
    d = diff[...] * transport_step
    d_wide = jnp.concatenate([d] * (width // 128), axis=1)

    def columns(src, low, high):
        scale = d_wide * (1.0 / SECOND_SCALE)

        def split(j, c):
            fs, gs = [], []
            for q in range(2):
                i = low + 2 * j + q
                f = src[i]
                fs.append(scale * f)
                gs.append((-transport_step / FIRST_SCALE) * (north[i] * f))
            f_high, f_low = halves(jnp.concatenate(fs, 0))
            g_high, g_low = halves(jnp.concatenate(gs, 0))
            at = pl.ds(pl.multiple_of(j * 16, 16), 16)
            pieces[at, 0:width] = f_high
            pieces[at, width:2 * width] = f_low
            pieces[at, 2 * width:3 * width] = g_high
            pieces[at, 3 * width:4 * width] = g_low
            return c

        lax.fori_loop(0, (high - low) // 2, split, 0, unroll=2 if (high - low) % 4 == 0 else 1)
        count = (high - low) * 8
        across[0:count] = jnp.dot(pieces[0:count], band[...], preferred_element_type=jnp.float32)

    def change(src, i, low, n):
        lap = sixth_center * src[i, :, :n]
        grad = None
        for k in range(1, 4):
            ahead, behind = src[i + k, :, :n], src[i - k, :, :n]
            lap = lap + sixth_second[k - 1] * (ahead + behind)
            slope = (sixth_first[k - 1] * transport_step) * (
                east[i + k, :, :n] * ahead - east[i - k, :, :n] * behind)
            grad = slope if grad is None else grad + slope
        col = across[pl.ds(pl.multiple_of((i - low) * 8, 8), 8), :n]
        return col + (d_wide[:, :n] * lap - grad)

    columns(start, 3, wide - 3)

    def first(i, c):
        one[i] = start[i] + change(start, i, 3, width)
        return c

    lax.fori_loop(3, wide - 3, first, 0, unroll=math.gcd(wide - 6, 4))
    columns(one, 6, wide - 6)

    def second(i, c):
        two[i] = 0.75 * start[i] + 0.25 * (one[i] + change(one, i, 6, width))
        return c

    lax.fori_loop(6, wide - 6, second, 0, unroll=math.gcd(wide - 12, 4))
    columns(two, 9, wide - 9)
    ids = tile * 8 + lax.broadcasted_iota(jnp.int32, (8, cols), 0)
    is_species = ids < fields - 1

    def third(i, c):
        value = start[i, :, :cols] * (1.0 / 3.0) + (2.0 / 3.0) * (
            two[i, :, :cols] + change(two, i, 9, cols))
        out[i - HALO] = jnp.where(is_species, jnp.maximum(value, 0.0), value)
        return c

    lax.fori_loop(9, wide - 9, third, 0, unroll=math.gcd(rows, 4))


def band_matrix(width):
    here = np.arange(width)
    lag = (here[:, None] - here[None, :]) % width
    second = np.where(lag == 0, round(sixth_center * SECOND_SCALE), 0)
    first = np.zeros((width, width))
    for k in range(1, 4):
        ahead, behind = lag == k, lag == width - k
        second = np.where(ahead | behind, round(sixth_second[k - 1] * SECOND_SCALE), second)
        weight = round(sixth_first[k - 1] * FIRST_SCALE)
        first = np.where(ahead, weight, np.where(behind, -weight, first))
    return jnp.asarray(np.concatenate([second, second, first, first], 0), jnp.bfloat16)


def transport(main, top, bottom, side, vectors, diff_at, fields):
    rows, layers, cols = main.shape
    wide = rows + 2 * HALO
    gap = side.shape[2]
    width = cols + gap
    uv_tile = fields // 8
    band = band_matrix(width)
    by = lambda r, n: pl.BlockSpec((r, 8, n), lambda t: (0, t, 0))
    uv = lambda r, n: pl.BlockSpec((r, 8, n), lambda t: (0, uv_tile, 0))
    return pl.pallas_call(
        functools.partial(transport_kernel, fields),
        grid=(layers // 8,),
        in_specs=[by(rows, cols), by(HALO, cols), by(HALO, cols), by(wide, gap),
                  pl.BlockSpec((8, 128), lambda t: (diff_at + t, 0)),
                  pl.BlockSpec(band.shape, lambda t: (0, 0)),
                  uv(rows, cols), uv(HALO, cols), uv(HALO, cols), uv(wide, gap)],
        out_specs=by(rows, cols),
        out_shape=jax.ShapeDtypeStruct(main.shape, jnp.float32),
        scratch_shapes=[pltpu.VMEM((wide, 8, width), jnp.float32) for _ in range(5)]
        + [pltpu.VMEM(((wide - 6) * 8, 4 * width), jnp.bfloat16),
           pltpu.VMEM(((wide - 6) * 8, width), jnp.float32)],
        name="transport",
    )(main, top, bottom, side, vectors, band, main, top, bottom, side)


GROUP = 16
PITCH = GROUP + 1
LANES = 128


def chemistry_kernel(reactions, species, order, counts, pair, rates, warming, state, gain, out, warm_out,
                     held, gained, progress, table, steps, staged, sems, *losses):
    rows, layers, cols = state.shape
    per_row = cols // TILE
    tiles = rows * per_row
    warm_row = species
    span = progress.shape[0] // GROUP
    depth = span // 8 * 8
    half = table.shape[0] // 2
    blocks = layers // 8

    progress[...] = jnp.zeros_like(progress)
    table[...] = jnp.zeros_like(table)
    high, low = halves(gain[...])
    table[0:species, 0:reactions] = high
    table[half:half + species, 0:reactions] = low
    for loss in losses:
        loss[...] = jnp.zeros_like(loss)

    def at(field):
        return pl.ds(field * PITCH, GROUP)

    def handle(g, c):
        ids = [order[g * GROUP + t] for t in range(GROUP)]
        numbers = [counts[t] for t in ids]
        places = [(t // per_row, pl.ds(pl.multiple_of((t % per_row) * TILE, TILE), TILE)) for t in ids]
        turn_count = functools.reduce(jnp.maximum, numbers)
        for t in range(GROUP):
            r, lanes = places[t]
            steps[t:t + 1, :] = jnp.full((1, LANES), numbers[t].astype(jnp.float32))
            for f in range(blocks):
                held[pl.ds(f * 8 * PITCH + t, 8, stride=PITCH)] = state[r, f * 8:(f + 1) * 8, lanes]

        def advance(s, c):
            heat = jnp.tanh(held[at(warm_row)])
            for r in range(reactions):
                first = pl.ds(pair[r], GROUP)
                second = pl.ds(pair[reactions + r], GROUP)
                a = jnp.broadcast_to(rates[r:r + 1, :], (GROUP, LANES))
                e = jnp.broadcast_to(rates[reactions + r:reactions + r + 1, :], (GROUP, LANES))
                weight = jnp.broadcast_to(rates[2 * reactions + r:2 * reactions + r + 1, :], (GROUP, LANES))
                rate = jnp.exp2(a + e * heat)
                ca, cb = held[first], held[second]
                qa, qb = rate * ca, rate * cb
                progress[pl.ds(r, GROUP, stride=span)] = qa * (weight * cb)
                n = 2 * (r % (len(losses) // 2))
                losses[n][first] += qb
                losses[n + 1][second] += qa
            for q in range(GROUP // 2):
                p = jnp.concatenate([progress[pl.ds((2 * q + t) * span, depth)] for t in range(2)], 1)
                both = jnp.dot(table[...], p.astype(jnp.bfloat16), preferred_element_type=jnp.float32)
                total = both[:half] + both[half:]
                for t in range(2):
                    for f in range(blocks):
                        gained[pl.ds(f * 8 * PITCH + 2 * q + t, 8, stride=PITCH)] = (
                            total[f * 8:(f + 1) * 8, t * TILE:(t + 1) * TILE])
            number = steps[...]
            h = chemistry_span / number
            active = s.astype(jnp.float32) < number
            change = jnp.zeros((GROUP, LANES), jnp.float32)
            for j in range(species):
                x = held[at(j)]
                destroyed = functools.reduce(jnp.add, [loss[at(j)] for loss in losses])
                for loss in losses:
                    loss[at(j)] = jnp.zeros((GROUP, LANES), jnp.float32)
                updated = (x + h * gained[at(j)]) / (1.0 + h * destroyed)
                change = change + warming[j] * (updated - x)
                held[at(j)] = jnp.where(active, updated, x)
            w = held[at(warm_row)]
            held[at(warm_row)] = jnp.where(active, w + change, w)
            return c

        lax.fori_loop(0, turn_count, advance, 0)
        for t in range(GROUP):
            for f in range(0, warm_row + 1, 8):
                n = min(8, warm_row + 1 - f)
                staged[pl.ds(((ids[t] % per_row) * (warm_row + 1) + f) * rows + ids[t] // per_row, n, stride=rows)] = (
                    held[pl.ds(f * PITCH + t, n, stride=PITCH)])
        return c

    lax.fori_loop(0, tiles // GROUP, handle, 0)
    height = (warm_row + 1) * rows
    copies = []
    for n in range(per_row):
        lanes = pl.ds(n * TILE, TILE)
        copies.append(pltpu.make_async_copy(
            staged.at[pl.ds(n * height, warm_row * rows)], out.at[:, lanes], sems.at[0, n]))
        copies.append(pltpu.make_async_copy(
            staged.at[pl.ds(n * height + warm_row * rows, rows)], warm_out.at[:, lanes], sems.at[1, n]))
    for copy in copies:
        copy.start()
    for copy in copies:
        copy.wait()


LOSSES = 6


def chemistry(state, order, counts, pair, rates, warming, gain):
    rows, layers, cols = state.shape
    species, reactions = gain.shape
    depth = -(-reactions // 16) * 16
    smem = pl.BlockSpec(memory_space=pltpu.SMEM)
    vmem = pl.BlockSpec(memory_space=pltpu.VMEM)
    block = pltpu.VMEM((layers * PITCH, LANES), jnp.float32)
    return pl.pallas_call(
        functools.partial(chemistry_kernel, reactions, species),
        in_specs=[smem, smem, smem, vmem, smem, vmem, vmem],
        out_specs=[pl.BlockSpec(memory_space=pl.ANY)] * 2,
        out_shape=[jax.ShapeDtypeStruct((species * rows, cols), jnp.float32),
                   jax.ShapeDtypeStruct((rows, cols), jnp.float32)],
        scratch_shapes=[block, block,
                        pltpu.VMEM((GROUP * (depth + 1), LANES), jnp.float32),
                        pltpu.VMEM((2 * -(-layers // 16) * 16, depth), jnp.bfloat16),
                        pltpu.VMEM((GROUP, LANES), jnp.float32),
                        pltpu.VMEM((cols // TILE * (species + 1) * rows, TILE), jnp.float32),
                        pltpu.SemaphoreType.DMA((2, cols // TILE))]
        + [block] * LOSSES,
        name="chemistry",
    )(order, counts, pair, rates, warming, state, gain)


def spread_weights(reactions):
    golden = (math.sqrt(5.0) - 1.0) / 2.0
    return jnp.asarray(np.exp2((np.arange(reactions) * golden) % 1.0), jnp.float32)


def by_count(counts):
    tiles = counts.shape[0]
    ids = jnp.arange(tiles, dtype=jnp.int32)
    key = counts * tiles + ids
    rank = jnp.sum((key[None, :] < key[:, None]).astype(jnp.int32), 1)
    return jnp.sum(jnp.where(rank[:, None] == ids[None, :], ids[:, None], 0), 0)


def body(component_density, scaled_thermal_state, leading_direction_flow, trailing_direction_flow,
         spreading_coefficient, colliding_pair, natural_exponent_scaler, arrhenius_energy,
         stoichiometric_output, formation_warming, explicit_increments):
    species, rows, cols = component_density.shape
    fields = species + 1
    layers = up8(fields + 2)
    bundle = jnp.concatenate(
        [component_density, scaled_thermal_state[None], leading_direction_flow[None],
         trailing_direction_flow[None]], 0)
    bundle = jnp.pad(bundle, ((0, layers - fields - 2), (0, 0), (0, 0)))
    main = jnp.transpose(bundle, (1, 0, 2))

    first_cols = jnp.transpose(main[:, :, :HALO], (0, 2, 1))
    last_cols = jnp.transpose(main[:, :, cols - HALO:], (0, 2, 1))
    top, bottom, left, right = exchange(main, first_cols, last_cols)
    gap = jnp.zeros((rows + 2 * HALO, 128 - 2 * HALO, layers), jnp.float32)
    side = jnp.transpose(jnp.concatenate([right, gap, left], 1), (0, 2, 1))
    spread = jnp.broadcast_to(jnp.pad(spreading_coefficient, (0, layers - fields))[:, None], (layers, 128))
    clipped = transport(main, top, bottom, side, spread, 0, fields)
    scale = 1.0 / math.log(2.0)
    weight = spread_weights(arrhenius_energy.shape[0])
    rates = jnp.concatenate([natural_exponent_scaler * scale, arrhenius_energy * scale, weight])
    rates = jnp.broadcast_to(rates[:, None], (rates.shape[0], LANES))
    pair = jnp.concatenate([colliding_pair[:, 0], colliding_pair[:, 1]]) * PITCH
    reacted, warm = chemistry(clipped, by_count(explicit_increments), explicit_increments, pair, rates,
                              formation_warming, stoichiometric_output.T / weight)
    return reacted.reshape(species, rows, cols), warm


def solution(mesh):
    return jax.shard_map(
        body,
        mesh=mesh,
        in_specs=(
            P(None, "gx", "grp"),
            P("gx", "grp"),
            P("gx", "grp"),
            P("gx", "grp"),
            P(),
            P(),
            P(),
            P(),
            P(),
            P(),
            P(("grp", "gx")),
        ),
        out_specs=(P(None, "gx", "grp"), P("gx", "grp")),
        check_vma=False,
    )
```

profile of v0, /device:TPU:0, one launch (start us, length us, event | category | flops | bytes accessed | tf_op | source)
XLA Modules:
  0.0 108.9 jit_solution(5747483143176875368)
XLA Ops:
  0.6 0.0 copy-start.3
  0.7 2.5 %copy.20 = f32[53,32,256]{2,0,1:T(8,128)S(1)} copy(f32[53,32,256]{2,1,0:T(8,128)} %param.13) | data formatting | bytes 3473408 | tf_op args[0]
  3.3 0.2 maximum_bitcast_fusion.main.uv_main
  3.5 0.3 slice_bitcast_fusion
  3.8 0.9 copy-done
  4.7 1.0 copy.21.first_cols
  5.8 1.0 copy.22.last_cols
  6.8 23.8 %halo.1 = (f32[9,56,256]{2,1,0:T(8,128)}, f32[9,56,256]{2,1,0:T(8,128)}, f32[50,9,56]{2,1,0:T(8,128)}, f32[50,9,56]{2,1,0:T(8,128)}) custom-call(f32[32,56,256]{2,1,0:T(8,128)} %copy-done, f32[32,9,56]{2,1,0:T(8,128)} %copy.21.first_cols, f32[32,9,56]{2,1,0:T(8,128)} %copy.22.last_cols), custom_call_target="tpu_custom_call" | custom-call | tf_op jit(solution)/shard_map/halo/pallas_call | solution.py:67
  30.6 1.5 %copy.23 = f32[50,9,56]{1,2,0:T(8,128)S(1)} copy(f32[50,9,56]{2,1,0:T(8,128)} %get-tuple-element.10) | data formatting | bytes 201600 | tf_op jit(solution)/shard_map/halo/pallas_call | solution.py:67
  32.2 0.5 copy.24
  32.7 0.1 pad.6.clone
  32.8 1.6 %maximum_bitcast_fusion.1.side.uv_side = f32[50,56,128]{2,1,0:T(8,128)} fusion(f32[50,9,56]{1,2,0:T(8,128)S(1)} %copy.24, f32[50,9,56]{1,2,0:T(8,128)S(1)} %copy.23, f32[128]{0:T(128)S(1)} %pad.6.clone), kind=kLoop, calls=%fused_computation.1 | loop fusion | flops 716800 | bytes 1635712 | tf_op jit(solution)/shard_map/transpose | solution.py:382
  34.4 0.7 broadcast_in_dim.49.diff
  35.1 0.0 copy-start.2
  35.1 0.0 copy-start.7
  35.1 0.0 copy-start.11
  35.1 35.2 %transport.1.state = f32[32,56,256]{2,1,0:T(8,128)} custom-call(f32[32,56,256]{2,1,0:T(8,128)} %copy-done, f32[9,56,256]{2,1,0:T(8,128)} %get-tuple-element.8.top.uv_top, f32[9,56,256]{2,1,0:T(8,128)} %get-tuple-element.9.bottom.uv_bottom, f32[50,56,128]{2,1,0:T(8,128)} %maximum_bitcast_fusion.1.side.uv_side, f32[56,128]{1,0:T(8,128)} %broadcast_in_dim.49.diff, ...), custom_call_target="tpu_custom_call" | custom-call | tf_op jit(solution)/shard_map/transport/pallas_call | solution.py:210
  70.3 0.1 pad_maximum_fusion
  70.4 1.0 broadcast_in_dim.44.rates
  71.4 0.7 add_multiply_fusion.pair
  72.1 0.6 multiply_bitcast_fusion.gain
  72.7 0.2 convert_reduce_fusion
  72.9 0.6 select_reduce_fusion.order
  73.5 35.4 %chemistry.1 = (f32[1696,256]{1,0:T(8,128)}, f32[32,256]{1,0:T(8,128)}) custom-call(s32[64]{0:T(128)} %select_reduce_fusion.order, s32[64]{0:T(128)} %counts.1, s32[650]{0:T(1024)} %add_multiply_fusion.pair, f32[975,128]{1,0:T(8,128)} %broadcast_in_dim.44.rates, f32[53]{0:T(128)} %warming.1, f32[32,56,256]{2,1,0:T(8,128)} %transport.1.state, ...), custom_call_target="tpu_custom_call" | custom-call | tf_op jit(solution)/shard_map/chemistry/pallas_call | solution.py:336
  (29 shorter events, 0.1 us)
Async XLA Ops:
  0.6 2.5 %copy-start.3 = (f32[32,256]{1,0:T(8,128)S(1)}, f32[32,256]{1,0:T(8,128)}, u32[]{:S(2)}) copy-start(f32[32,256]{1,0:T(8,128)} %param.14) | copy-start | bytes 98308
  0.6 2.6 %copy-start.4 = (f32[32,256]{1,0:T(8,128)S(1)}, f32[32,256]{1,0:T(8,128)}, u32[]{:S(2)}) copy-start(f32[32,256]{1,0:T(8,128)} %param.15) | copy-start | bytes 98308
  0.7 2.6 %copy-start.5 = (f32[32,256]{1,0:T(8,128)S(1)}, f32[32,256]{1,0:T(8,128)}, u32[]{:S(2)}) copy-start(f32[32,256]{1,0:T(8,128)} %param.16) | copy-start | bytes 98308
  3.5 1.2 %copy-start = (f32[32,56,256]{2,1,0:T(8,128)}, f32[32,56,256]{2,1,0:T(8,128)S(1)}, u32[]{:S(2)}) copy-start(f32[32,56,256]{2,1,0:T(8,128)S(1)} %maximum_bitcast_fusion.main.uv_main) | copy-start | bytes 5505028
  30.6 1.6 %copy-start.1 = (f32[50,9,56]{2,1,0:T(8,128)S(1)}, f32[50,9,56]{2,1,0:T(8,128)}, u32[]{:S(2)}) copy-start(f32[50,9,56]{2,1,0:T(8,128)} %get-tuple-element.11) | copy-start | bytes 302404
  32.8 1.6 %copy-start.12 = (f32[54]{0:T(128)S(1)}, f32[54]{0:T(128)}, u32[]{:S(2)}) copy-start(f32[54]{0:T(128)} %param.17) | copy-start | bytes 652
  35.0 35.2 %copy-start.9 = (f32[325]{0:T(512)S(1)}, f32[325]{0:T(512)}, u32[]{:S(2)}) copy-start(f32[325]{0:T(512)} %param.20) | copy-start | bytes 3904
  35.0 35.2 %copy-start.10 = (f32[325]{0:T(512)S(1)}, f32[325]{0:T(512)}, u32[]{:S(2)}) copy-start(f32[325]{0:T(512)} %param.19) | copy-start | bytes 3904
  35.0 35.2 %copy-start.8 = (f32[325]{0:T(512)S(1)}, f32[325]{0:T(512)}, u32[]{:S(2)}) copy-start(f32[325]{0:T(512)} %constant.16.clone) | copy-start | bytes 3904
  35.0 36.3 %copy-start.6 = (s32[325,2]{0,1:T(2,128)S(1)}, s32[325,2]{0,1:T(2,128)}, u32[]{:S(2)}) copy-start(s32[325,2]{0,1:T(2,128)} %param.18) | copy-start | bytes 7804
  35.1 37.0 %copy-start.2 = (f32[325,53]{0,1:T(8,128)S(1)}, f32[325,53]{0,1:T(8,128)}, u32[]{:S(2)}) copy-start(f32[325,53]{0,1:T(8,128)} %param.21) | copy-start | bytes 206704
  35.1 37.0 %copy-start.7 = (f32[325]{0:T(512)S(1)}, f32[325]{0:T(512)}, u32[]{:S(2)}) copy-start(f32[325]{0:T(512)} %constant.19) | copy-start | bytes 3904
  35.1 37.6 %copy-start.11 = (s32[64]{0:T(128)S(1)}, s32[64]{0:T(128)}, u32[]{:S(2)}) copy-start(s32[64]{0:T(128)} %counts.1) | copy-start | bytes 772
where the time goes:
time: 108 us; the launch traced here: 109 us
  Pallas kernels  94.3 us (87%)
  local copies, waits for them, and re-layouts  9.79 us (9%)
  other arithmetic  3.94 us (4%)
    pallas_call x1, Pallas kernels, chemistry(): pl.pallas_call(functools.partial(chemistry_kernel, reactions, species), i...  35.4 us
    pallas_call x1, Pallas kernels, transport(): pl.pallas_call(functools.partial(transport_kernel, fields), grid=(layers...  35.2 us
    pallas_call x1, Pallas kernels, exchange(): pl.pallas_call(functools.partial(halo_kernel, sizes), in_specs=[anywhere]...  23.8 us
    unnamed x27, local copies, waits for them, and re-layouts  3.48 us

commit v1 on v0

v1 whole, which is shorter than its diff:
```python
import functools
import math

import jax
import jax.numpy as jnp
import numpy as np
from jax import lax
from jax.experimental import pallas as pl
from jax.experimental.pallas import tpu as pltpu
from jax.sharding import PartitionSpec as P

TILE = 128
FIRST_SCALE = 60.0
SECOND_SCALE = 180.0
transport_step = 0.4
chemistry_span = 0.5
sixth_first = (0.75, -0.15, 1.0 / 60.0)
sixth_second = (1.5, -0.15, 1.0 / 90.0)
sixth_center = -49.0 / 18.0


def up8(n):
    return -(-n // 8) * 8


REACH = 3
SLOT = 4
LANES = 128


def halves(value):
    high = value.astype(jnp.bfloat16)
    return high, (value - high.astype(jnp.float32)).astype(jnp.bfloat16)


def advect_kernel(fields, sizes, density, warm, leading, trailing, spread, band, out,
                  start, one, two, east, north, pieces, across, packed, landed, flows, send, recv):
    n_grp, n_gx = sizes
    g, x = lax.axis_index("grp"), lax.axis_index("gx")
    rows, cols = warm.shape
    parts = cols // LANES
    tiles = start.shape[0] // parts
    species = fields - 1
    last = fields // 8
    up, down = (g, lax.rem(x + n_gx - 1, n_gx)), (g, lax.rem(x + 1, n_gx))
    left, right = (lax.rem(g + n_grp - 1, n_grp), x), (lax.rem(g + 1, n_grp), x)
    barrier = pltpu.get_barrier_semaphore()
    for place in (up, down, left, right):
        pl.semaphore_signal(barrier, inc=1, device_id=place, device_id_type=pl.DeviceIdType.MESH)

    lane = lax.broadcasted_iota(jnp.int32, (8, LANES), 1)
    row_of = lane // SLOT
    slot = lane % SLOT

    def at(row, count=1):
        return pl.ds(pl.multiple_of(row * 8, 8), count * 8)

    def spread_out(read, t, sub):
        for q in range(rows // 8):
            for h in range(parts):
                start[t * parts + h, pl.ds((REACH + q * 8) * 8 + sub, 8, stride=8), :] = read(q, h)

    def of_density(f):
        return lambda q, h: density[pl.ds(pl.multiple_of(f * rows + q * 8, 8), 8), h * LANES:(h + 1) * LANES]

    def of_plane(ref):
        return lambda q, h: ref[q * 8:(q + 1) * 8, h * LANES:(h + 1) * LANES]

    def copies(s, t):
        held = (start, one, two)[s]
        both = pl.ds(t * parts, parts)
        plan = [
            (held.at[both, pl.ds(REACH * 8, REACH * 8)], held.at[both, pl.ds((REACH + rows) * 8, REACH * 8)], up),
            (held.at[both, pl.ds(rows * 8, REACH * 8)], held.at[both, pl.ds(0, REACH * 8)], down),
            (packed.at[s, t, 0], landed.at[s, t, 1], left),
            (packed.at[s, t, 1], landed.at[s, t, 0], right),
        ]
        return [pltpu.make_async_remote_copy(
            src_ref=src, dst_ref=dst, send_sem=send.at[s, t, n], recv_sem=recv.at[s, t, n],
            device_id=place, device_id_type=pl.DeviceIdType.MESH) for n, (src, dst, place) in enumerate(plan)]

    def pack(s, t):
        held = (start, one, two)[s]
        first = jnp.zeros((8, LANES), jnp.float32)
        final = jnp.zeros((8, LANES), jnp.float32)
        for i in range(rows):
            mine = row_of == i
            first = jnp.where(mine, pltpu.roll(held[t * parts, at(REACH + i), :], (SLOT * i) % LANES, 1), first)
            final = jnp.where(mine, pltpu.roll(held[t * parts + parts - 1, at(REACH + i), :],
                                               (SLOT * i + REACH) % LANES, 1), final)
        packed[s, t, 0] = first
        packed[s, t, 1] = final
        for copy in copies(s, t):
            copy.start()

    for f in range(last * 8, species):
        spread_out(of_density(f), last, f % 8)
    for n, ref in enumerate((warm, leading, trailing)):
        spread_out(of_plane(ref), last, (species + n) % 8)
    pl.semaphore_wait(barrier, 4)
    pack(0, last)

    def prepare(t, c):
        for sub in range(8):
            spread_out(of_density(t * 8 + sub), t, sub)
        pack(0, t)
        return c

    lax.fori_loop(0, last, prepare, 0)

    for i in range(rows):
        for h in range(parts):
            lanes = slice(h * LANES, (h + 1) * LANES)
            east[h, at(REACH + i), :] = jnp.broadcast_to(leading[i:i + 1, lanes], (8, LANES))
            north[h, at(i), :] = jnp.broadcast_to(trailing[i:i + 1, lanes], (8, LANES))

    def arrive(s, t):
        for copy in copies(s, t):
            copy.wait_recv()

    arrive(0, last)
    u_sub, v_sub = fields % 8, (fields + 1) % 8
    for r in (*range(REACH), *range(REACH + rows, 2 * REACH + rows)):
        for h in range(parts):
            east[h, at(r), :] = jnp.broadcast_to(
                start[last * parts + h, pl.ds(r * 8 + u_sub, 1), :], (8, LANES))
    for side in range(2):
        flow = jnp.broadcast_to(landed[0, last, side, pl.ds(v_sub, 1), :], (8, LANES))
        for k in range(1, REACH + 1):
            inside = (slot >= REACH - k) & (slot < REACH) if side == 0 else slot < k
            weight = (1.0 if side == 0 else -1.0) * transport_step * sixth_first[k - 1]
            flows[side * REACH + k - 1] = jnp.where(inside, weight * flow, 0.0)

    def stage(s):
        held, fresh = (start, one, two)[s], (one, two, None)[s]

        def tile(n, c):
            t = lax.rem(n + last, tiles)

            @pl.when(n > 0 if s == 0 else n >= 0)
            def _():
                arrive(s, t)

            d = spread[at(t), :] * transport_step
            scale = d * (1.0 / SECOND_SCALE)

            def split(j, c):
                for h in range(parts):
                    fs, gs = [], []
                    for q in range(2):
                        i = 2 * j + q
                        f = held[t * parts + h, at(REACH + i), :]
                        fs.append(scale * f)
                        gs.append((-transport_step / FIRST_SCALE) * (north[h, at(i), :] * f))
                    f_high, f_low = halves(jnp.concatenate(fs, 0))
                    g_high, g_low = halves(jnp.concatenate(gs, 0))
                    place = pl.ds(pl.multiple_of(j * 16, 16), 16)
                    for m, piece in enumerate((f_high, f_low, g_high, g_low)):
                        pieces[place, m * cols + h * LANES:m * cols + (h + 1) * LANES] = piece
                return c

            lax.fori_loop(0, rows // 2, split, 0, unroll=4)
            across[...] = jnp.dot(pieces[...], band[...], preferred_element_type=jnp.float32)

            borders = []
            for side in range(2):
                halo = landed[s, t, side]
                total = None
                for k in range(1, REACH + 1):
                    inside = (slot >= REACH - k) & (slot < REACH) if side == 0 else slot < k
                    part = (jnp.where(inside, sixth_second[k - 1] * d, 0.0) + flows[side * REACH + k - 1]) * halo
                    if k < REACH:
                        part = pltpu.roll(part, (k - REACH) % LANES if side == 0 else REACH - k, 1)
                    total = part if total is None else total + part
                borders.append(total)
            ids = t * 8 + lax.broadcasted_iota(jnp.int32, (8, LANES), 0)

            def update(b, c):
                for h in range(parts):
                    lanes = slice(h * LANES, (h + 1) * LANES)
                    f = [held[t * parts + h, at(b * 8 + m), :] for m in range(8 + 2 * REACH)]
                    gs = [east[h, at(b * 8 + m), :] * f[m] for m in range(8 + 2 * REACH)]
                    for r in range(8):
                        i = b * 8 + r
                        m = r + REACH
                        lap = sixth_center * f[m]
                        grad = None
                        for k in range(1, REACH + 1):
                            lap = lap + sixth_second[k - 1] * (f[m + k] + f[m - k])
                            slope = (sixth_first[k - 1] * transport_step) * (gs[m + k] - gs[m - k])
                            grad = slope if grad is None else grad + slope
                        change = across[at(i), lanes] + (d * lap - grad)
                        if h == 0:
                            change = change + jnp.where(
                                lane < REACH, pltpu.roll(borders[0], lax.rem(LANES - SLOT * i, LANES), 1), 0.0)
                        if h == parts - 1:
                            change = change + jnp.where(
                                lane >= LANES - REACH,
                                pltpu.roll(borders[1], lax.rem(2 * LANES - REACH - SLOT * i, LANES), 1), 0.0)
                        if s == 0:
                            fresh[t * parts + h, at(REACH + i), :] = f[m] + change
                        elif s == 1:
                            fresh[t * parts + h, at(REACH + i), :] = (
                                0.75 * start[t * parts + h, at(REACH + i), :] + 0.25 * (f[m] + change))
                        else:
                            value = start[t * parts + h, at(REACH + i), :] * (1.0 / 3.0) + (2.0 / 3.0) * (f[m] + change)
                            out[t * parts + h, at(i), :] = jnp.where(ids < species, jnp.maximum(value, 0.0), value)
                return c

            lax.fori_loop(0, rows // 8, update, 0)
            if s < 2:
                pack(s + 1, t)
            return c

        lax.fori_loop(0, tiles, tile, 0)

    for s in range(3):
        stage(s)

    def finish(t, c):
        for s in range(3):
            for copy in copies(s, t):
                copy.wait_send()
        return c

    lax.fori_loop(0, tiles, finish, 0)


def band_matrix(width):
    here = np.arange(width)
    lag = here[:, None] - here[None, :]
    second = np.where(lag == 0, round(sixth_center * SECOND_SCALE), 0)
    first = np.zeros((width, width))
    for k in range(1, REACH + 1):
        ahead, behind = lag == k, lag == -k
        second = np.where(ahead | behind, round(sixth_second[k - 1] * SECOND_SCALE), second)
        weight = round(sixth_first[k - 1] * FIRST_SCALE)
        first = np.where(ahead, weight, np.where(behind, -weight, first))
    return jnp.asarray(np.concatenate([second, second, first, first], 0), jnp.bfloat16)


def advect(density, warm, leading, trailing, spread):
    species, rows, cols = density.shape
    fields = species + 1
    tiles = (fields + 2) // 8
    if (fields + 2) % 8 or rows * SLOT > LANES or cols % LANES or rows % 8:
        raise ValueError("unsupported sizes")
    parts = cols // LANES
    sizes = (lax.axis_size("grp"), lax.axis_size("gx"))
    vmem = pl.BlockSpec(memory_space=pltpu.VMEM)
    wide = pltpu.VMEM((tiles * parts, (rows + 2 * REACH) * 8, LANES), jnp.float32)
    band = band_matrix(cols)
    return pl.pallas_call(
        functools.partial(advect_kernel, fields, sizes),
        in_specs=[vmem] * 6,
        out_specs=vmem,
        out_shape=jax.ShapeDtypeStruct((tiles * parts, rows * 8, LANES), jnp.float32),
        scratch_shapes=[wide, wide, wide,
                        pltpu.VMEM((parts, (rows + 2 * REACH) * 8, LANES), jnp.float32),
                        pltpu.VMEM((parts, rows * 8, LANES), jnp.float32),
                        pltpu.VMEM((rows * 8, 4 * cols), jnp.bfloat16),
                        pltpu.VMEM((rows * 8, cols), jnp.float32),
                        pltpu.VMEM((3, tiles, 2, 8, LANES), jnp.float32),
                        pltpu.VMEM((3, tiles, 2, 8, LANES), jnp.float32),
                        pltpu.VMEM((2 * REACH, 8, LANES), jnp.float32),
                        pltpu.SemaphoreType.DMA((3, tiles, 4)),
                        pltpu.SemaphoreType.DMA((3, tiles, 4))],
        compiler_params=pltpu.CompilerParams(collective_id=0, has_side_effects=True),
        name="advect",
    )(density.reshape(species * rows, cols), warm, leading, trailing, spread, band)


GROUP = 16
PITCH = GROUP + 1


def chemistry_kernel(reactions, species, order, counts, pair, rates, warming, state, gain, out, warm_out,
                     held, gained, progress, table, steps, staged, sems, *losses):
    rows, cols = warm_out.shape
    layers = state.shape[0] * LANES // cols * 8
    per_row = cols // TILE
    tiles = rows * per_row
    warm_row = species
    span = progress.shape[0] // GROUP
    depth = span // 8 * 8
    half = table.shape[0] // 2
    blocks = layers // 8

    progress[...] = jnp.zeros_like(progress)
    table[...] = jnp.zeros_like(table)
    high, low = halves(gain[...])
    table[0:species, 0:reactions] = high
    table[half:half + species, 0:reactions] = low
    for loss in losses:
        loss[...] = jnp.zeros_like(loss)

    def at(field):
        return pl.ds(field * PITCH, GROUP)

    def handle(g, c):
        ids = [order[g * GROUP + t] for t in range(GROUP)]
        numbers = [counts[t] for t in ids]
        places = [(t % per_row, pl.ds(pl.multiple_of(t // per_row * 8, 8), 8)) for t in ids]
        turn_count = functools.reduce(jnp.maximum, numbers)
        for t in range(GROUP):
            part, at_row = places[t]
            steps[t:t + 1, :] = jnp.full((1, LANES), numbers[t].astype(jnp.float32))
            for f in range(blocks):
                held[pl.ds(f * 8 * PITCH + t, 8, stride=PITCH)] = state[f * per_row + part, at_row, :]

        def advance(s, c):
            heat = jnp.tanh(held[at(warm_row)])
            for r in range(reactions):
                first = pl.ds(pair[r], GROUP)
                second = pl.ds(pair[reactions + r], GROUP)
                a = jnp.broadcast_to(rates[r:r + 1, :], (GROUP, LANES))
                e = jnp.broadcast_to(rates[reactions + r:reactions + r + 1, :], (GROUP, LANES))
                weight = jnp.broadcast_to(rates[2 * reactions + r:2 * reactions + r + 1, :], (GROUP, LANES))
                rate = jnp.exp2(a + e * heat)
                ca, cb = held[first], held[second]
                qa, qb = rate * ca, rate * cb
                progress[pl.ds(r, GROUP, stride=span)] = qa * (weight * cb)
                n = 2 * (r % (len(losses) // 2))
                losses[n][first] += qb
                losses[n + 1][second] += qa
            for q in range(GROUP // 2):
                p = jnp.concatenate([progress[pl.ds((2 * q + t) * span, depth)] for t in range(2)], 1)
                both = jnp.dot(table[...], p.astype(jnp.bfloat16), preferred_element_type=jnp.float32)
                total = both[:half] + both[half:]
                for t in range(2):
                    for f in range(blocks):
                        gained[pl.ds(f * 8 * PITCH + 2 * q + t, 8, stride=PITCH)] = (
                            total[f * 8:(f + 1) * 8, t * TILE:(t + 1) * TILE])
            number = steps[...]
            h = chemistry_span / number
            active = s.astype(jnp.float32) < number
            change = jnp.zeros((GROUP, LANES), jnp.float32)
            for j in range(species):
                x = held[at(j)]
                destroyed = functools.reduce(jnp.add, [loss[at(j)] for loss in losses])
                for loss in losses:
                    loss[at(j)] = jnp.zeros((GROUP, LANES), jnp.float32)
                updated = (x + h * gained[at(j)]) / (1.0 + h * destroyed)
                change = change + warming[j] * (updated - x)
                held[at(j)] = jnp.where(active, updated, x)
            w = held[at(warm_row)]
            held[at(warm_row)] = jnp.where(active, w + change, w)
            return c

        lax.fori_loop(0, turn_count, advance, 0)
        for t in range(GROUP):
            for f in range(0, warm_row + 1, 8):
                n = min(8, warm_row + 1 - f)
                staged[pl.ds(((ids[t] % per_row) * (warm_row + 1) + f) * rows + ids[t] // per_row, n, stride=rows)] = (
                    held[pl.ds(f * PITCH + t, n, stride=PITCH)])
        return c

    lax.fori_loop(0, tiles // GROUP, handle, 0)
    height = (warm_row + 1) * rows
    copies = []
    for n in range(per_row):
        lanes = pl.ds(n * TILE, TILE)
        copies.append(pltpu.make_async_copy(
            staged.at[pl.ds(n * height, warm_row * rows)], out.at[:, lanes], sems.at[0, n]))
        copies.append(pltpu.make_async_copy(
            staged.at[pl.ds(n * height + warm_row * rows, rows)], warm_out.at[:, lanes], sems.at[1, n]))
    for copy in copies:
        copy.start()
    for copy in copies:
        copy.wait()


LOSSES = 6


def chemistry(state, order, counts, pair, rates, warming, gain, rows, cols):
    species, reactions = gain.shape
    layers = state.shape[0] * LANES // cols * 8
    depth = -(-reactions // 16) * 16
    smem = pl.BlockSpec(memory_space=pltpu.SMEM)
    vmem = pl.BlockSpec(memory_space=pltpu.VMEM)
    block = pltpu.VMEM((layers * PITCH, LANES), jnp.float32)
    return pl.pallas_call(
        functools.partial(chemistry_kernel, reactions, species),
        in_specs=[smem, smem, smem, vmem, smem, vmem, vmem],
        out_specs=[pl.BlockSpec(memory_space=pl.ANY)] * 2,
        out_shape=[jax.ShapeDtypeStruct((species * rows, cols), jnp.float32),
                   jax.ShapeDtypeStruct((rows, cols), jnp.float32)],
        scratch_shapes=[block, block,
                        pltpu.VMEM((GROUP * (depth + 1), LANES), jnp.float32),
                        pltpu.VMEM((2 * -(-layers // 16) * 16, depth), jnp.bfloat16),
                        pltpu.VMEM((GROUP, LANES), jnp.float32),
                        pltpu.VMEM((cols // TILE * (species + 1) * rows, TILE), jnp.float32),
                        pltpu.SemaphoreType.DMA((2, cols // TILE))]
        + [block] * LOSSES,
        name="chemistry",
    )(order, counts, pair, rates, warming, state, gain)


def spread_weights(reactions):
    golden = (math.sqrt(5.0) - 1.0) / 2.0
    return jnp.asarray(np.exp2((np.arange(reactions) * golden) % 1.0), jnp.float32)


def by_count(counts):
    tiles = counts.shape[0]
    ids = jnp.arange(tiles, dtype=jnp.int32)
    key = counts * tiles + ids
    rank = jnp.sum((key[None, :] < key[:, None]).astype(jnp.int32), 1)
    return jnp.sum(jnp.where(rank[:, None] == ids[None, :], ids[:, None], 0), 0)


def body(component_density, scaled_thermal_state, leading_direction_flow, trailing_direction_flow,
         spreading_coefficient, colliding_pair, natural_exponent_scaler, arrhenius_energy,
         stoichiometric_output, formation_warming, explicit_increments):
    species, rows, cols = component_density.shape
    layers = up8(species + 3)
    spread = jnp.broadcast_to(jnp.pad(spreading_coefficient, (0, layers - species - 1))[:, None], (layers, LANES))
    clipped = advect(component_density, scaled_thermal_state, leading_direction_flow, trailing_direction_flow, spread)
    scale = 1.0 / math.log(2.0)
    weight = spread_weights(arrhenius_energy.shape[0])
    rates = jnp.concatenate([natural_exponent_scaler * scale, arrhenius_energy * scale, weight])
    rates = jnp.broadcast_to(rates[:, None], (rates.shape[0], LANES))
    pair = jnp.concatenate([colliding_pair[:, 0], colliding_pair[:, 1]]) * PITCH
    reacted, warm = chemistry(clipped, by_count(explicit_increments), explicit_increments, pair, rates,
                              formation_warming, stoichiometric_output.T / weight, rows, cols)
    return reacted.reshape(species, rows, cols), warm


def solution(mesh):
    return jax.shard_map(
        body,
        mesh=mesh,
        in_specs=(
            P(None, "gx", "grp"),
            P("gx", "grp"),
            P("gx", "grp"),
            P("gx", "grp"),
            P(),
            P(),
            P(),
            P(),
            P(),
            P(),
            P(("grp", "gx")),
        ),
        out_specs=(P(None, "gx", "grp"), P("gx", "grp")),
        check_vma=False,
    )
```

time: 108 us -> 77.5 us (0.72)
  the two profiles are of different devices: /device:TPU:0 before, /device:TPU:9 now
where the time goes in v1:
time: 77.5 us; the launch traced here: 77.2 us
  Pallas kernels  68.3 us (88%)
  other arithmetic  5.17 us (7%)
  local copies, waits for them, and re-layouts  3.11 us (4%)
    pallas_call x1, Pallas kernels, chemistry(): pl.pallas_call(functools.partial(chemistry_kernel, reactions, species), i...  37 us
    pallas_call x1, Pallas kernels, advect(): pl.pallas_call(functools.partial(advect_kernel, fields, sizes), in_specs=...  31.3 us

profile of v1, /device:TPU:9, one launch (start us, length us, event | category | flops | bytes accessed | tf_op | source)
XLA Modules:
  0.0 77.2 jit_solution(12576221059872770167)
XLA Ops:
  0.6 0.7 pad.4
  1.3 0.7 iota_add_fusion
  1.9 0.2 convert_reduce_fusion
  2.1 0.7 select_reduce_fusion.order
  2.8 0.8 %slice_reduce_fusion.1 = (s32[325]{0:T(512)S(1)}, s32[325]{0:T(512)S(1)}) fusion(s32[325,2]{0,1:T(2,128)} %param.18), kind=kLoop, calls=%fused_computation.7 | loop fusion | bytes 5200 | tf_op jit(solution)/shard_map/slice | solution.py:424
  3.6 0.7 add_multiply_fusion.pair
  4.3 0.7 broadcast_multiply_fusion
  5.0 0.8 pad_maximum_fusion
  5.7 0.7 broadcast_in_dim.15.spread
  6.4 1.5 %multiply_bitcast_fusion.gain = f32[53,325]{1,0:T(8,128)} fusion(f32[325,53]{0,1:T(8,128)} %param.21, f32[325]{0:T(512)} %constant.18), kind=kLoop, calls=%fused_computation | loop fusion | flops 17225 | bytes 139100 | tf_op jit(solution)/shard_map/div | solution.py:426
  7.9 1.0 %broadcast_in_dim.14.rates = f32[975,128]{1,0:T(8,128)} broadcast(f32[975]{0:T(1024)S(1)} %pad_maximum_fusion), dimensions={0} | broadcast | bytes 503100 | tf_op jit(solution)/shard_map/broadcast_in_dim | solution.py:423
  8.9 31.3 %advect.1.state = f32[14,256,128]{2,1,0:T(8,128)} custom-call(f32[1696,256]{1,0:T(8,128)} %bitcast.4, f32[32,256]{1,0:T(8,128)} %warm.1, f32[32,256]{1,0:T(8,128)} %leading.1, f32[32,256]{1,0:T(8,128)} %trailing.1, f32[56,128]{1,0:T(8,128)} %broadcast_in_dim.15.spread, bf16[1024,256]{1,0:T(8,128)(2,1)} %constant.14.clone.band), custom_call_target="tpu_custom_call" | custom-call | tf_op jit(solution)/shard_map/advect/pallas_call | solution.py:253
  40.2 37.0 %chemistry.1 = (f32[1696,256]{1,0:T(8,128)}, f32[32,256]{1,0:T(8,128)}) custom-call(s32[64]{0:T(128)} %select_reduce_fusion.order, s32[64]{0:T(128)} %counts.1, s32[650]{0:T(1024)} %add_multiply_fusion.pair, f32[975,128]{1,0:T(8,128)} %broadcast_in_dim.14.rates, f32[53]{0:T(128)} %warming.1, f32[14,256,128]{2,1,0:T(8,128)} %advect.1.state, ...), custom_call_target="tpu_custom_call" | custom-call | tf_op jit(solution)/shard_map/chemistry/pallas_call | solution.py:383
